TPU v7x, 32 devices: a whole 2x2x4 slice. The times are simulated.
32 devices in a mesh: group: 2 (over y), fsdp: 16 (over z, x, core).
Axes of the slice: x: 2, y: 2, z: 4, core: 2. Of those that a mesh axis runs over, the one named last changes fastest.
Arguments:
- teacher_rows: bfloat16 [20480, 2048], P(('group', 'fsdp')), may hold values from -6 to 6
- student_rows: bfloat16 [20480, 1024], P(('group', 'fsdp')), may hold values from -6 to 6
- counts: int32 [32], P(('group', 'fsdp')), may hold values from 213 to 640, as said below
- teacher_weight: bfloat16 [2048, 4096], P(None, ('group', 'fsdp')), may hold values from -0.125 to 0.125
- teacher_bias: float32 [4096], replicated, may hold values from -6 to 6
- teacher_gain: float32 [4096], replicated, may hold values from 0.1 to 1.9
- teacher_head: float32 [4096], replicated, may hold values from -0.09375 to 0.09375
- cross_weight: bfloat16 [1024, 1024], replicated, may hold values from -0.1875 to 0.1875
- cross_bias: float32 [1024], replicated, may hold values from -3 to 3
- out_weight: float32 [1024], replicated, may hold values from -0.1875 to 0.1875
Outputs:
- grad_cross: float32 [1024, 1024], P('fsdp')
- grad_bias: float32 [1024], replicated
- grad_out: float32 [1024], replicated
Inputs may be any that keep to these rules, and one draw needn't show every extreme that they name: counts[i] live impressions fill the first slots of shard i, the rest of its 640 slots are padding.
All inputs are finite; a program needn't handle non-finite values.
Results may differ from a plain program's by a relative error of at most 0.00035.
The roundings to bfloat16 on the way count: a program that leaves them out, or rounds other values in their place, can miss the bound.
Values may be sent and summed in bfloat16 or wider, within the bound.
A program may use at most 128 MiB of HBM per device.

v0:
```python
import math

import jax
import jax.numpy as jnp
from jax import lax
from jax.sharding import PartitionSpec as P

epsilon = 1e-06


def shards(
    teacher_rows,
    student_rows,
    counts,
    teacher_weight,
    teacher_bias,
    teacher_gain,
    teacher_head,
    cross_weight,
    cross_bias,
    out_weight,
):
    row_count = teacher_rows.shape[0]
    width_s = cross_weight.shape[0]
    group_count = lax.axis_size("group")
    fsdp_count = lax.axis_size("fsdp")
    shard_count = group_count * fsdp_count
    loss_scale = math.sqrt(width_s / (row_count * shard_count))
    preact = jnp.dot(
        teacher_rows,
        lax.all_gather(teacher_weight, ("group", "fsdp"), axis=1, tiled=True),
        preferred_element_type=jnp.float32,
    )
    preact = preact + teacher_bias
    meansq = jnp.mean(preact * preact, axis=-1, keepdims=True)
    normed = preact * lax.rsqrt(meansq + epsilon) * teacher_gain
    teacher_logit = jnp.sum(jax.nn.silu(normed) * teacher_head, axis=-1)
    cross = jnp.dot(student_rows, cross_weight, preferred_element_type=jnp.float32) + cross_bias
    inputs_f = student_rows.astype(jnp.float32)
    mixed = inputs_f * cross + inputs_f
    student_logit = jnp.sum(mixed * out_weight, axis=-1)
    live_rows = (jnp.arange(row_count, dtype=jnp.int32) < counts[0]).astype(jnp.float32)
    error = (student_logit - teacher_logit) * live_rows * loss_scale
    dcross = error[:, None] * out_weight[None, :] * inputs_f
    dcross_half = dcross.astype(jnp.bfloat16)
    term_b = jnp.sum(dcross, axis=0)
    term_o = jnp.sum(error[:, None] * mixed, axis=0)
    term_w = lax.dot_general(
        student_rows, dcross_half, (((0,), (0,)), ((), ())), preferred_element_type=jnp.float32
    )
    totals = lax.psum((term_w, term_b, term_o), "group")
    grad_cross = lax.psum_scatter(totals[0], "fsdp", scatter_dimension=0, tiled=True)
    small_sums = lax.psum((totals[1], totals[2]), "fsdp")
    return (grad_cross, small_sums[0], small_sums[1])


def solution(mesh):
    in_specs = (
        P(("group", "fsdp"), None),
        P(("group", "fsdp"), None),
        P(("group", "fsdp")),
        P(None, ("group", "fsdp")),
        P(),
        P(),
        P(),
        P(),
        P(),
        P(),
    )
    out_specs = (P("fsdp", None), P(), P())
    return jax.shard_map(shards, mesh=mesh, in_specs=in_specs, out_specs=out_specs, check_vma=False)
```

profile of v0, /device:TPU:0, one launch (start us, length us, event | category | flops | bytes accessed | tf_op | source)
XLA Modules:
  0.0 307.7 jit_solution(12406359859207324828)
XLA Ops:
  7.2 0.0 copy-start
  7.2 0.0 all-gather.2.cloned.1.call-start
  7.2 0.7 all-gather.2.cloned.1.call-update
  7.9 0.0 reduce-scatter.4.cloned.1.call-start
  8.6 0.0 copy-start.2
  8.6 5.6 %multiply_reduce_fusion.3 = (f32[640]{0:T(1024)S(1)}, f32[640,1024]{1,0:T(8,128)}) fusion(f32[1024]{0:T(1024)} %param.19, f32[1024]{0:T(1024)} %param.18, bf16[640,1024]{1,0:T(8,128)(2,1)} %param.11, bf16[1024,1024]{1,0:T(8,128)(2,1)} %param.17), kind=kOutput, calls=%fused_computation.7 | convolution fusion | flops 1346108800 | bytes 6040064 | tf_op jit(solution)/shard_map/dot_general | solution.py:38
  14.2 0.0 copy-start.3
  14.2 0.0 copy-start.4
  14.2 146.2 %all-gather.2.cloned.1.call-done = bf16[2048,4096]{1,0:T(8,128)(2,1)} async-done(((bf16[2048,128]{1,0:T(8,128)(2,1)}), bf16[2048,4096]{1,0:T(8,128)(2,1)}) %all-gather.2.cloned.1.call-update) | async-done | bytes 16777232 | tf_op jit(solution)/shard_map/all_gather | solution.py:31
  160.4 0.0 copy-done
  160.4 0.0 copy-done.2
  160.4 14.0 %multiply_reduce_fusion.1 = (f32[640]{0:T(1024)S(1)}, f32[640,4096]{1,0:T(8,128)S(1)}) fusion(f32[4096]{0:T(1024)S(1)} %copy-done.2, bf16[640,2048]{1,0:T(8,128)(2,1)S(1)} %copy-done, bf16[2048,4096]{1,0:T(8,128)(2,1)} %all-gather.2.cloned.1.call-done), kind=kOutput, calls=%fused_computation.1 | convolution fusion | flops 10745281536 | bytes 29903360 | tf_op jit(solution)/shard_map/dot_general | solution.py:29
  174.5 0.0 copy-done.3
  174.5 0.0 copy-done.4
  174.5 0.0 copy-start.1
  174.5 0.0 copy-start.5
  174.5 4.1 %multiply_reduce_fusion = f32[640]{0:T(1024)S(1)} fusion(f32[640,4096]{1,0:T(8,128)S(1)} %get-tuple-element.18, f32[4096]{0:T(1024)S(1)} %copy-done.3, f32[4096]{0:T(1024)S(1)} %copy-done.4, f32[640]{0:T(1024)S(1)} %add_rsqrt_fusion, f32[4096]{0:T(1024)S(1)} %copy-done.2), kind=kLoop, calls=%fused_computation | loop fusion | flops 23592320 | bytes 10540032 | tf_op jit(solution)/shard_map/reduce_sum | solution.py:37
  178.6 0.0 copy-done.1
  178.6 0.0 copy-done.5
  178.7 3.9 %convolution_bitcast_fusion = f32[1024,1024]{0,1:T(8,128)} fusion(bf16[640,1024]{1,0:T(8,128)(2,1)S(1)} %copy-done.1, f32[640]{0:T(1024)S(1)} %select_multiply_fusion, f32[1024]{0:T(1024)S(1)} %copy-done.5), kind=kOutput, calls=%fused_computation.8 | convolution fusion | flops 1344798720 | bytes 5511680 | tf_op jit(solution)/shard_map/dot_general | solution.py:48
  182.6 5.3 %copy.15 = f32[1024,1024]{1,0:T(8,128)} copy(f32[1024,1024]{0,1:T(8,128)} %convolution_bitcast_fusion) | data formatting | bytes 8388608
  187.9 0.0 reduce-scatter.4.cloned.1.call-update
  188.0 0.0 all-reduce.4.cloned.1.call-start
  188.0 71.0 %reduce-scatter.4.cloned.1.call-done = f32[64,1024]{1,0:T(8,128)} async-done(((f32[1024,1024]{1,0:T(8,128)}), f32[64,1024]{1,0:T(8,128)}) %reduce-scatter.4.cloned.1.call-update) | async-done | bytes 262160
  259.0 1.9 copy.16
  261.0 0.0 all-reduce.4.cloned.1.call-update
  261.0 2.7 multiply_reduce_fusion.2
  263.7 5.0 %all-reduce.1 = (f32[1024]{0:T(1024)S(1)}, f32[1024]{0:T(1024)S(1)}) all-reduce(f32[1024]{0:T(1024)S(1)} %get-tuple-element.10, f32[1024]{0:T(1024)S(1)} %get-tuple-element.9), channel_id=1, replica_groups=mesh['group'=2,'fsdp'=16] {'group'}, use_global_device_ids=true, to_apply=%region_6.7 | all-reduce | flops 2048 | bytes 16384 | tf_op jit(solution)/shard_map/psum | solution.py:51
  268.7 30.6 %all-reduce = (f32[1024]{0:T(1024)}, f32[1024]{0:T(1024)}) all-reduce(f32[1024]{0:T(1024)S(1)} %get-tuple-element.13, f32[1024]{0:T(1024)S(1)} %get-tuple-element.14), channel_id=1, replica_groups=mesh['group'=2,'fsdp'=16] {'fsdp'}, use_global_device_ids=true, to_apply=%region_7.8 | all-reduce | flops 2048 | bytes 16384 | tf_op jit(solution)/shard_map/psum | solution.py:53
  299.3 0.0 all-reduce.4.cloned.1.call-done
  299.3 1.9 copy.14
  (2 shorter events, 0.0 us)
Async XLA Ops:
  7.2 153.2 %copy-start = (bf16[640,2048]{1,0:T(8,128)(2,1)S(1)}, bf16[640,2048]{1,0:T(8,128)(2,1)}, u32[]{:S(2)}) copy-start(bf16[640,2048]{1,0:T(8,128)(2,1)} %param.10) | copy-start | bytes 7864324
  7.2 153.2 %all-gather.2.cloned.1.call-start = ((), (), s32[]{:S(2)}) async-start(), calls=%async_computation.1 | async-start | bytes 17301504 | tf_op jit(solution)/shard_map/all_gather | solution.py:31
  7.9 251.1 %reduce-scatter.4.cloned.1.call-start = ((), (), s32[]{:S(2)}) async-start(), calls=%async_computation.3 | async-start | bytes 4456448
  8.6 151.8 %copy-start.2 = (f32[4096]{0:T(1024)S(1)}, f32[4096]{0:T(1024)}, u32[]{:S(2)}) copy-start(f32[4096]{0:T(1024)} %param.14) | copy-start | bytes 49156
  14.2 160.2 %copy-start.3 = (f32[4096]{0:T(1024)S(1)}, f32[4096]{0:T(1024)}, u32[]{:S(2)}) copy-start(f32[4096]{0:T(1024)} %param.16) | copy-start | bytes 49156
  14.2 160.2 %copy-start.4 = (f32[4096]{0:T(1024)S(1)}, f32[4096]{0:T(1024)}, u32[]{:S(2)}) copy-start(f32[4096]{0:T(1024)} %param.15) | copy-start | bytes 49156
  174.5 4.2 %copy-start.1 = (bf16[640,1024]{1,0:T(8,128)(2,1)S(1)}, bf16[640,1024]{1,0:T(8,128)(2,1)}, u32[]{:S(2)}) copy-start(bf16[640,1024]{1,0:T(8,128)(2,1)} %param.11) | copy-start | bytes 3932164
  174.5 4.2 %copy-start.5 = (f32[1024]{0:T(1024)S(1)}, f32[1024]{0:T(1024)}, u32[]{:S(2)}) copy-start(f32[1024]{0:T(1024)} %param.19) | copy-start | bytes 12292
  188.0 111.3 %all-reduce.4.cloned.1.call-start = ((), (), s32[]{:S(2)}) async-start(), calls=%async_computation.2 | async-start | bytes 1048576 | tf_op jit(solution)/shard_map/psum | solution.py:51
Sparse Core Ops, SparseCore 0:
  10.8 149.4 all-gather.1
  188.1 70.9 reduce-scatter.3
  261.3 27.7 all-reduce.3
where the time goes:
time: 308 us
  waiting for transfers between devices  218 us (71%)
  blocking collectives  35.6 us (12%)
  matrix products  23.6 us (8%)
  between operations  14.5 us (5%)
  local copies, waits for them, and re-layouts  9.25 us (3%)
  other arithmetic  6.82 us (2%)
    all_gather x1, waiting for transfers between devices, shards(): lax.all_gather(teacher_weight, ('group', 'fsdp'), axis=1, tiled=True)  146 us
    unnamed x4, waiting for transfers between devices  71.7 us
    psum x1, blocking collectives, shards(): small_sums = lax.psum((totals[1], totals[2]), 'fsdp')  30.6 us
    dot_general x1, matrix products, shards(): jnp.dot(teacher_rows, lax.all_gather(teacher_weight, ('group', 'fsdp'), a...  14 us
    unnamed x15, local copies, waits for them, and re-layouts  9.25 us
  transfers between devices with their start and end apart: 3, of which 2 were waited for; matrix products, arithmetic and copies ran while one was open for 3% of the time, Pallas kernels for 0%

commit v1 on v0

--- a/solution.py
+++ b/solution.py
@@ -1,8 +1,11 @@
+import functools
 import math
 
 import jax
 import jax.numpy as jnp
 from jax import lax
+from jax.experimental import pallas as pl
+from jax.experimental.pallas import tpu as pltpu
 from jax.sharding import PartitionSpec as P
 
 epsilon = 1e-06
@@ -54,6 +57,401 @@
     return (grad_cross, small_sums[0], small_sums[1])
 
 
+MESH = pl.DeviceIdType.MESH
+LANES = 128
+PAIRS = 2
+
+
+def fused(fsdp_count, rp, t_ref, s_ref, live_ref, w_ref, bias_ref, gain_ref, head_ref, cw_ref, cb_ref, ow_ref,
+          out_ref, small_ref,
+          wbuf, rows, xs, cw, pre, ssq, gains, heads, mixed, msg1, in1, msg2, in2, rr, er, xt, dbuf,
+          tw, r1, s1, r2, tt, r3, fin, r4, sb, rb, rz, lsem, ssem, rsem):
+    g = lax.axis_index("group")
+    f = lax.axis_index("fsdp")
+    core = lax.rem(f, 2)
+    x = lax.rem(lax.div(f, 2), 2)
+    z = lax.div(f, 4)
+    nz = fsdp_count // 4
+    row_count, fin_width = t_ref.shape
+    width_s = s_ref.shape[1]
+    block = width_s // fsdp_count
+    half_rows = block // 2
+    rt = row_count // LANES
+    units = bias_ref.shape[0] * LANES
+    parts = 2 * PAIRS
+    pw = width_s // parts
+
+    def at(y_, z_, x_, c_):
+        return (y_, (z_ * 2 + x_) * 2 + c_)
+
+    partner = at(g, z, x, 1 - core)
+    xn = at(g, z, 1 - x, core)
+    yn = at(1 - g, z, x, core)
+    barrier = pltpu.get_barrier_semaphore()
+    peers = [partner, xn, yn] + [at(g, lax.rem(z + k, nz), x, core) for k in range(1, nz)]
+    for peer in peers:
+        pl.semaphore_signal(barrier, inc=1, device_id=peer, device_id_type=MESH)
+
+    locals_ = []
+    for i, (a, b) in enumerate([
+        (s_ref, xs.at[pl.ds(0, row_count)]),
+        (cw_ref, cw),
+        (w_ref, wbuf.at[0]),
+        (t_ref, rows.at[pl.ds(0, row_count)]),
+    ]):
+        cp = pltpu.make_async_copy(a, b, lsem.at[i])
+        cp.start()
+        locals_.append(cp)
+    pl.semaphore_wait(barrier, len(peers))
+
+    sends = []
+
+    def send(a, b, device):
+        i = len(sends)
+        cp = pltpu.make_async_remote_copy(
+            src_ref=a, dst_ref=b, send_sem=ssem.at[i], recv_sem=rsem.at[i], device_id=device, device_id_type=MESH
+        )
+        cp.start()
+        sends.append(cp)
+        return cp
+
+    def slot(dx, dy, dz):
+        return (dx * 2 + dy) * nz + dz
+
+    order = [1] + list(range(nz - 1, 1, -1))
+    xin, yin, zin, din = {}, {}, {}, {}
+    xin[0] = send(w_ref, wbuf.at[slot(1, 0, 0)], xn)
+    yin[0] = send(w_ref, wbuf.at[slot(0, 1, 0)], yn)
+    for k in order:
+        zin[k] = send(w_ref, wbuf.at[slot(0, 0, k)], at(g, lax.rem(z + nz - k, nz), x, core))
+    rows_in = send(t_ref, rows.at[pl.ds(row_count, row_count)], partner)
+    xs_in = send(s_ref, xs.at[pl.ds(row_count, row_count)], partner)
+
+    depth = fin_width // 2
+
+    def forward(k):
+        xin[k].wait_recv()
+        a = send(wbuf.at[slot(1, 0, k), pl.ds(0, depth)], wbuf.at[slot(1, 1, k), pl.ds(0, depth)], yn)
+        yin[k].wait_recv()
+        b = send(wbuf.at[slot(0, 1, k), pl.ds(depth, depth)], wbuf.at[slot(1, 1, k), pl.ds(depth, depth)], xn)
+        din[k] = (a, b)
+
+    def relay(k):
+        zin[k].wait_recv()
+        xin[k] = send(wbuf.at[slot(0, 0, k)], wbuf.at[slot(1, 0, k)], xn)
+        yin[k] = send(wbuf.at[slot(0, 0, k)], wbuf.at[slot(0, 1, k)], yn)
+
+    eye = lax.broadcasted_iota(jnp.int32, (LANES, LANES), 0) == lax.broadcasted_iota(jnp.int32, (LANES, LANES), 1)
+
+    def to_row(col):
+        return jnp.sum(jnp.where(eye, col, 0.0), axis=0, keepdims=True)
+
+    def to_col(row):
+        return jnp.sum(jnp.where(eye, row, 0.0), axis=1, keepdims=True)
+
+    def tile(t):
+        return pl.ds(pl.multiple_of(t * LANES, LANES), LANES)
+
+    ssq[...] = jnp.zeros_like(ssq)
+    for ref in (msg1, msg2, er, rr):
+        ref[...] = jnp.zeros_like(ref)
+    msg1[pl.ds(3 * rp, rt), :] = live_ref[...]
+
+    locals_[0].wait()
+    locals_[1].wait()
+    ow = ow_ref[...]
+
+    def student(t, carry):
+        xt_ = xs[tile(t), :]
+        cross = jnp.dot(xt_, cw[...], preferred_element_type=jnp.float32) + cb_ref[...]
+        xf = xt_.astype(jnp.float32)
+        m = xf * cross + xf
+        mixed[tile(t), :] = m
+        msg1[pl.ds(2 * rp + t, 1), :] = to_row(jnp.sum(m * ow, axis=1, keepdims=True))
+        return carry
+
+    lax.fori_loop(0, rt, student, 0)
+    locals_[2].wait()
+    locals_[3].wait()
+
+    mt = 2 * LANES
+
+    def project(dx, dy, dz):
+        s = slot(dx, dy, dz)
+        y_ = g if dy == 0 else 1 - g
+        x_ = x if dx == 0 else 1 - x
+        index = y_ * fsdp_count + (lax.rem(z + dz, nz) * 2 + x_) * 2 + core
+        gains[pl.ds(s, 1), :] = gain_ref[index] * 0.5
+        heads[pl.ds(s, 1), :] = head_ref[index]
+        bias = bias_ref[index]
+
+        def step(t, carry):
+            ds = pl.ds(pl.multiple_of(t * mt, mt), mt)
+            p = jnp.dot(rows[ds, :], wbuf[s], preferred_element_type=jnp.float32) + bias
+            pre[s, ds, :] = p
+            ssq[ds, :] += p * p
+            return carry
+
+        lax.fori_loop(0, 2 * row_count // mt, step, 0)
+
+    forward(0)
+    rows_in.wait_recv()
+    project(0, 0, 0)
+    relay(order[0])
+    project(1, 0, 0)
+    project(0, 1, 0)
+
+    xs_in.wait_recv()
+    pick = (
+        lax.broadcasted_iota(jnp.int32, (block, 2 * block), 1)
+        == lax.broadcasted_iota(jnp.int32, (block, 2 * block), 0) + core * block
+    )
+    pick = jnp.where(pick, 1.0, 0.0).astype(jnp.bfloat16)
+    for j in range(fsdp_count // 2):
+        xt[pl.ds(j * block, block), :] = lax.dot_general(
+            pick, xs[:, pl.ds(j * 2 * block, 2 * block)], (((1,), (1,)), ((), ())), preferred_element_type=jnp.float32
+        ).astype(jnp.bfloat16)
+
+    previous = 0
+    for n, k in enumerate(order):
+        if n > 0:
+            relay(k)
+        project(0, 0, k)
+        for cp in din[previous]:
+            cp.wait_recv()
+        project(1, 1, previous)
+        forward(k)
+        project(1, 0, k)
+        project(0, 1, k)
+        previous = k
+    for cp in din[previous]:
+        cp.wait_recv()
+    project(1, 1, previous)
+
+    for h in range(2):
+        def squares(t, carry, h=h):
+            col = jnp.sum(ssq[tile(h * rt + t), :], axis=1, keepdims=True)
+            msg1[pl.ds(h * rp + t, 1), :] = to_row(col)
+            return carry
+
+        lax.fori_loop(0, rt, squares, 0)
+    m1 = send(msg1, in1, partner)
+    m1.wait_recv()
+    for h in range(2):
+        total = msg1[pl.ds(h * rp, rp), :] + in1[pl.ds((1 - h) * rp, rp), :]
+        rr[pl.ds(h * rp, rp), :] = lax.rsqrt(total * (1.0 / units) + epsilon)
+
+    for h in range(2):
+        def logits(t, carry, h=h):
+            r = to_col(rr[pl.ds(h * rp + t, 1), :])
+            acc = jnp.zeros((LANES, LANES), jnp.float32)
+            for s in range(4 * nz):
+                v = pre[s, tile(h * rt + t), :] * r * gains[pl.ds(s, 1), :]
+                acc += (v * jnp.tanh(v) + v) * heads[pl.ds(s, 1), :]
+            msg2[pl.ds(h * rp + t, 1), :] = to_row(jnp.sum(acc, axis=1, keepdims=True))
+            return carry
+
+        lax.fori_loop(0, rt, logits, 0)
+    m2 = send(msg2, in2, partner)
+    m2.wait_recv()
+    for h, src in ((0, msg1), (1, in1)):
+        teacher = msg2[pl.ds(h * rp, rp), :] + in2[pl.ds((1 - h) * rp, rp), :]
+        er[pl.ds(h * rp, rp), :] = (src[pl.ds(2 * rp, rp), :] - teacher) * src[pl.ds(3 * rp, rp), :]
+
+    sb[...] = jnp.zeros_like(sb)
+
+    def own(t, carry):
+        e = to_col(er[pl.ds(t, 1), :])
+        d = e * ow * xs[tile(t), :].astype(jnp.float32)
+        dbuf[tile(t), :] = d.astype(jnp.bfloat16)
+        sb[0, pl.ds(0, 1), :] += jnp.sum(d, axis=0, keepdims=True)
+        sb[0, pl.ds(1, 1), :] += jnp.sum(e * mixed[tile(t), :], axis=0, keepdims=True)
+        return carry
+
+    lax.fori_loop(0, rt, own, 0)
+    c0 = send(sb.at[0], rb.at[0], partner)
+
+    def other(t, carry):
+        e = to_col(er[pl.ds(rp + t, 1), :])
+        d = e * ow * xs[tile(rt + t), :].astype(jnp.float32)
+        dbuf[tile(rt + t), :] = d.astype(jnp.bfloat16)
+        return carry
+
+    lax.fori_loop(0, rt, other, 0)
+
+    def way(p):
+        return (g, x, yn, xn) if p % 2 == 0 else (x, g, xn, yn)
+
+    h1, h2, h3, h4 = {}, {}, {}, {}
+    for p in range(parts):
+        val = jnp.dot(xt[...], dbuf[:, pl.ds(p * pw, pw)], preferred_element_type=jnp.float32)
+        for z_ in range(nz):
+            for x_ in range(2):
+                for y_ in range(2):
+                    first, second = (y_, x_) if p % 2 == 0 else (x_, y_)
+                    offset = ((z_ * 2 + x_) * 2 + y_) * half_rows
+                    tw[p, first, second, z_] = val[offset:offset + half_rows, :]
+        first, second, n1, n2 = way(p)
+        h1[p] = send(tw.at[p, 1 - first], r1.at[p], n1)
+    c0.wait_recv()
+    sb[1] = sb[0] + rb[0]
+    c1 = send(sb.at[1], rb.at[1], xn)
+
+    def stage2(p):
+        first, second, n1, n2 = way(p)
+        h1[p].wait_recv()
+        s1[p] = tw[p, first] + r1[p]
+        h2[p] = send(s1.at[p, 1 - second], r2.at[p], n2)
+
+    def stage3(p):
+        first, second, n1, n2 = way(p)
+        h2[p].wait_recv()
+        tt[p] = s1[p, second] + r2[p]
+        h3[p] = []
+        for k in range(1, nz):
+            to = lax.rem(z + k, nz)
+            h3[p].append(send(tt.at[p, to], r3.at[p, k - 1], at(g, to, x, core)))
+
+    def stage4(p):
+        total = tt[p, z]
+        for k in range(nz - 1):
+            h3[p][k].wait_recv()
+            total = total + r3[p, k]
+        fin[p] = total
+        h4[p] = send(fin.at[p], r4.at[p], yn)
+        out_ref[pl.ds(pl.multiple_of(g * half_rows, half_rows), half_rows), pl.ds(p * pw, pw)] = total
+
+    for p in range(parts):
+        stage2(p)
+        if p == 1:
+            c1.wait_recv()
+            sb[2] = sb[1] + rb[1]
+            c2 = send(sb.at[2], rb.at[2], yn)
+    for p in range(parts):
+        stage3(p)
+        if p == 1:
+            c2.wait_recv()
+            sb[3] = sb[2] + rb[2]
+            rz[z] = sb[3]
+            cz = []
+            for k in range(1, nz):
+                to = lax.rem(z + k, nz)
+                cz.append(send(sb.at[3], rz.at[z], at(g, to, x, core)))
+    for p in range(parts):
+        stage4(p)
+    for cp in cz:
+        cp.wait_recv()
+    total = rz[0]
+    for k in range(1, nz):
+        total = total + rz[k]
+    small_ref[...] = total
+    for p in range(parts):
+        h4[p].wait_recv()
+        out_ref[pl.ds(pl.multiple_of((1 - g) * half_rows, half_rows), half_rows), pl.ds(p * pw, pw)] = r4[p]
+    for cp in sends:
+        cp.wait_send()
+
+
+def shards_fused(
+    teacher_rows,
+    student_rows,
+    counts,
+    teacher_weight,
+    teacher_bias,
+    teacher_gain,
+    teacher_head,
+    cross_weight,
+    cross_bias,
+    out_weight,
+):
+    row_count, fin_width = teacher_rows.shape
+    width_s = cross_weight.shape[0]
+    group_count = lax.axis_size("group")
+    fsdp_count = lax.axis_size("fsdp")
+    loss_scale = math.sqrt(width_s / (row_count * group_count * fsdp_count))
+    live = (jnp.arange(row_count, dtype=jnp.int32) < counts[0]).astype(jnp.float32) * loss_scale
+    rt = row_count // LANES
+    rp = -(-rt // 8) * 8
+    nz = fsdp_count // 4
+    block = width_s // fsdp_count
+    half_rows = block // 2
+    parts = 2 * PAIRS
+    pw = width_s // parts
+    slots = 4 * nz
+    f32, bf16 = jnp.float32, jnp.bfloat16
+    vm = pltpu.VMEM
+    split = lambda v: v.reshape(-1, 1, LANES)
+    anyspec = pl.BlockSpec(memory_space=pl.ANY)
+    vspec = pl.BlockSpec(memory_space=pltpu.VMEM)
+    grad, small = pl.pallas_call(
+        functools.partial(fused, fsdp_count, rp),
+        out_shape=(jax.ShapeDtypeStruct((block, width_s), f32), jax.ShapeDtypeStruct((8, width_s), f32)),
+        in_specs=[anyspec, anyspec, vspec, anyspec, vspec, vspec, vspec, anyspec, vspec, vspec],
+        out_specs=(vspec, vspec),
+        scratch_shapes=[
+            vm((slots, fin_width, LANES), bf16),
+            vm((2 * row_count, fin_width), bf16),
+            vm((2 * row_count, width_s), bf16),
+            vm((width_s, width_s), bf16),
+            vm((slots, 2 * row_count, LANES), f32),
+            vm((2 * row_count, LANES), f32),
+            vm((slots, LANES), f32),
+            vm((slots, LANES), f32),
+            vm((row_count, width_s), f32),
+            vm((4 * rp, LANES), f32),
+            vm((4 * rp, LANES), f32),
+            vm((2 * rp, LANES), f32),
+            vm((2 * rp, LANES), f32),
+            vm((2 * rp, LANES), f32),
+            vm((2 * rp, LANES), f32),
+            vm((width_s // 2, 2 * row_count), bf16),
+            vm((2 * row_count, width_s), bf16),
+            vm((parts, 2, 2, nz, half_rows, pw), f32),
+            vm((parts, 2, nz, half_rows, pw), f32),
+            vm((parts, 2, nz, half_rows, pw), f32),
+            vm((parts, nz, half_rows, pw), f32),
+            vm((parts, nz, half_rows, pw), f32),
+            vm((parts, nz - 1, half_rows, pw), f32),
+            vm((parts, half_rows, pw), f32),
+            vm((parts, half_rows, pw), f32),
+            vm((4, 8, width_s), f32),
+            vm((3, 8, width_s), f32),
+            vm((nz, 8, width_s), f32),
+            pltpu.SemaphoreType.DMA((4,)),
+            pltpu.SemaphoreType.DMA((SEMS,)),
+            pltpu.SemaphoreType.DMA((SEMS,)),
+        ],
+        compiler_params=pltpu.CompilerParams(
+            collective_id=0, has_side_effects=True, vmem_limit_bytes=60 * 1024 * 1024
+        ),
+    )(
+        teacher_rows, student_rows, live.reshape(rt, LANES), teacher_weight, split(teacher_bias), split(teacher_gain),
+        split(teacher_head), cross_weight, cross_bias[None, :], out_weight[None, :],
+    )
+    return (grad, small[0], small[1])
+
+
+SEMS = 64
+
+
+def fits(mesh, args):
+    rows, fin_width = args[0].shape
+    width_s = args[1].shape[1]
+    units = args[3].shape[1]
+    group_count, fsdp_count = mesh.shape["group"], mesh.shape["fsdp"]
+    devices = group_count * fsdp_count
+    return (
+        group_count == 2
+        and fsdp_count % 4 == 0
+        and fsdp_count >= 8
+        and fsdp_count <= 16
+        and units == devices * LANES
+        and (rows // devices) % LANES == 0
+        and (2 * width_s // fsdp_count) % LANES == 0
+        and width_s % (2 * PAIRS * LANES) == 0
+    )
+
+
 def solution(mesh):
     in_specs = (
         P(("group", "fsdp"), None),
@@ -68,4 +466,9 @@
         P(),
     )
     out_specs = (P("fsdp", None), P(), P())
-    return jax.shard_map(shards, mesh=mesh, in_specs=in_specs, out_specs=out_specs, check_vma=False)
+
+    def run(*args):
+        body = shards_fused if fits(mesh, args) else shards
+        return jax.shard_map(body, mesh=mesh, in_specs=in_specs, out_specs=out_specs, check_vma=False)(*args)
+
+    return run

time: 308 us -> 136 us (0.44)
  the two profiles are of different devices: /device:TPU:0 before, /device:TPU:24 now
where the time goes in v1:
time: 136 us; the launch traced here: 135 us
  Pallas kernels  130 us (96%)
  local copies, waits for them, and re-layouts  3.11 us (2%)
    pallas_call x1, Pallas kernels, shards_fused(): pl.pallas_call(functools.partial(fused, fsdp_count, rp), out_shape=(jax.S...  130 us

profile of v1, /device:TPU:24, one launch (start us, length us, event | category | flops | bytes accessed | tf_op | source)
XLA Modules:
  0.0 135.3 jit_solution(3017729206093347453)
XLA Ops:
  1.3 0.6 fusion.live_ref
  1.9 130.3 %shard_map.121 = (f32[64,1024]{1,0:T(8,128)}, f32[8,1024]{1,0:T(8,128)}) custom-call(bf16[640,2048]{1,0:T(8,128)(2,1)} %t_ref.1, bf16[640,1024]{1,0:T(8,128)(2,1)} %s_ref.1, f32[5,128]{1,0:T(8,128)} %fusion.live_ref, bf16[2048,128]{1,0:T(8,128)(2,1)} %w_ref.1, f32[32,1,128]{2,1,0:T(1,128)} %bitcast.9, f32[32,1,128]{2,1,0:T(1,128)} %bitcast.10, ...), custom_call_target="tpu_custom_call" | custom-call | tf_op jit(solution)/shard_map/pallas_call | solution.py:386
  132.1 1.4 %fusion.1 = (f32[1,1024]{1,0:T(1,128)}, f32[1,1024]{1,0:T(1,128)}) fusion(f32[8,1024]{1,0:T(8,128)} %get-tuple-element.6), kind=kLoop, calls=%fused_computation.2 | loop fusion | bytes 16384 | tf_op jit(solution)/shard_map/slice | solution.py:431
  133.6 1.7 %copy.15 = f32[64,1024]{1,0:T(8,128)} copy(f32[64,1024]{1,0:T(8,128)} %get-tuple-element.12) | data formatting | bytes 524288

commit v2 on v1

--- a/solution.py
+++ b/solution.py
@@ -59,7 +59,7 @@
 
 MESH = pl.DeviceIdType.MESH
 LANES = 128
-PAIRS = 2
+PAIRS = 4
 
 
 def fused(fsdp_count, rp, t_ref, s_ref, live_ref, w_ref, bias_ref, gain_ref, head_ref, cw_ref, cb_ref, ow_ref,
@@ -119,27 +119,48 @@
         return (dx * 2 + dy) * nz + dz
 
     order = [1] + list(range(nz - 1, 1, -1))
+    depth = fin_width // 2
     xin, yin, zin, din = {}, {}, {}, {}
-    xin[0] = send(w_ref, wbuf.at[slot(1, 0, 0)], xn)
-    yin[0] = send(w_ref, wbuf.at[slot(0, 1, 0)], yn)
-    for k in order:
-        zin[k] = send(w_ref, wbuf.at[slot(0, 0, k)], at(g, lax.rem(z + nz - k, nz), x, core))
+
+    def half(ref, h):
+        return ref.at[pl.ds(h * depth, depth)]
+
+    def piece(dx, dy, dz, h):
+        return wbuf.at[slot(dx, dy, dz), pl.ds(h * depth, depth)]
+
+    def zpeer(k):
+        return at(g, lax.rem(z + nz - k, nz), x, core)
+
+    for h in range(2):
+        xin[0, h] = send(half(w_ref, h), piece(1, 0, 0, h), xn)
+        yin[0, h] = send(half(w_ref, h), piece(0, 1, 0, h), yn)
+        zin[order[0], h] = send(half(w_ref, h), piece(0, 0, order[0], h), zpeer(order[0]))
+    for k in order[1:]:
+        for h in range(2):
+            zin[k, h] = send(half(w_ref, h), piece(0, 0, k, h), zpeer(k))
     rows_in = send(t_ref, rows.at[pl.ds(row_count, row_count)], partner)
     xs_in = send(s_ref, xs.at[pl.ds(row_count, row_count)], partner)
 
-    depth = fin_width // 2
-
-    def forward(k):
-        xin[k].wait_recv()
-        a = send(wbuf.at[slot(1, 0, k), pl.ds(0, depth)], wbuf.at[slot(1, 1, k), pl.ds(0, depth)], yn)
-        yin[k].wait_recv()
-        b = send(wbuf.at[slot(0, 1, k), pl.ds(depth, depth)], wbuf.at[slot(1, 1, k), pl.ds(depth, depth)], xn)
-        din[k] = (a, b)
-
-    def relay(k):
-        zin[k].wait_recv()
-        xin[k] = send(wbuf.at[slot(0, 0, k)], wbuf.at[slot(1, 0, k)], xn)
-        yin[k] = send(wbuf.at[slot(0, 0, k)], wbuf.at[slot(0, 1, k)], yn)
+    def diagonal(k, h):
+        lo, hi = pl.ds(h * depth, depth // 2), pl.ds(h * depth + depth // 2, depth // 2)
+        xin[k, h].wait_recv()
+        a = send(wbuf.at[slot(1, 0, k), lo], wbuf.at[slot(1, 1, k), lo], yn)
+        yin[k, h].wait_recv()
+        b = send(wbuf.at[slot(0, 1, k), hi], wbuf.at[slot(1, 1, k), hi], xn)
+        din[k, h] = (a, b)
+
+    def relay(k, h):
+        zin[k, h].wait_recv()
+        xin[k, h] = send(piece(0, 0, k, h), piece(1, 0, k, h), xn)
+        yin[k, h] = send(piece(0, 0, k, h), piece(0, 1, k, h), yn)
+
+    def arrived(k, h):
+        for cp in din[k, h]:
+            cp.wait_recv()
+
+    def along(k, h):
+        arrived(0, h)
+        din[k, h] = (send(piece(1, 1, 0, h), piece(1, 1, k, h), zpeer(k)),)
 
     eye = lax.broadcasted_iota(jnp.int32, (LANES, LANES), 0) == lax.broadcasted_iota(jnp.int32, (LANES, LANES), 1)
 
@@ -174,7 +195,7 @@
     locals_[2].wait()
     locals_[3].wait()
 
-    mt = 2 * LANES
+    mt = row_count
 
     def project(dx, dy, dz):
         s = slot(dx, dy, dz)
@@ -194,10 +215,13 @@
 
         lax.fori_loop(0, 2 * row_count // mt, step, 0)
 
-    forward(0)
+    lead = order[0]
+    for h in range(2):
+        diagonal(0, h)
+        relay(lead, h)
     rows_in.wait_recv()
     project(0, 0, 0)
-    relay(order[0])
+    along(lead, 0)
     project(1, 0, 0)
     project(0, 1, 0)
 
@@ -212,21 +236,42 @@
             pick, xs[:, pl.ds(j * 2 * block, 2 * block)], (((1,), (1,)), ((), ())), preferred_element_type=jnp.float32
         ).astype(jnp.bfloat16)
 
-    previous = 0
-    for n, k in enumerate(order):
-        if n > 0:
-            relay(k)
-        project(0, 0, k)
-        for cp in din[previous]:
-            cp.wait_recv()
-        project(1, 1, previous)
-        forward(k)
-        project(1, 0, k)
-        project(0, 1, k)
-        previous = k
-    for cp in din[previous]:
-        cp.wait_recv()
-    project(1, 1, previous)
+    along(lead, 1)
+    ready = [(1, 1, 0), (0, 0, lead)]
+    late = []
+    before = None
+    for k in order[1:]:
+        if before is not None:
+            diagonal(before, 0)
+        relay(k, 0)
+        if before is not None:
+            diagonal(before, 1)
+            ready += [(1, 0, before), (0, 1, before)]
+        else:
+            for h in range(2):
+                xin[lead, h].wait_recv()
+                yin[lead, h].wait_recv()
+            late += [(1, 0, lead), (0, 1, lead)]
+        for item in ready:
+            project(*item)
+        relay(k, 1)
+        ready = late + [(0, 0, k)]
+        late = []
+        before = k
+    diagonal(before, 0)
+    for item in ready:
+        project(*item)
+    for k in order[1:-1]:
+        for h in range(2):
+            arrived(k, h)
+        project(1, 1, k)
+    diagonal(before, 1)
+    project(1, 0, before)
+    project(0, 1, before)
+    for k in (lead, before):
+        for h in range(2):
+            arrived(k, h)
+        project(1, 1, k)
 
     for h in range(2):
         def squares(t, carry, h=h):
@@ -283,7 +328,8 @@
         return (g, x, yn, xn) if p % 2 == 0 else (x, g, xn, yn)
 
     h1, h2, h3, h4 = {}, {}, {}, {}
-    for p in range(parts):
+
+    def stage1(p):
         val = jnp.dot(xt[...], dbuf[:, pl.ds(p * pw, pw)], preferred_element_type=jnp.float32)
         for z_ in range(nz):
             for x_ in range(2):
@@ -293,9 +339,6 @@
                     tw[p, first, second, z_] = val[offset:offset + half_rows, :]
         first, second, n1, n2 = way(p)
         h1[p] = send(tw.at[p, 1 - first], r1.at[p], n1)
-    c0.wait_recv()
-    sb[1] = sb[0] + rb[0]
-    c1 = send(sb.at[1], rb.at[1], xn)
 
     def stage2(p):
         first, second, n1, n2 = way(p)
@@ -321,24 +364,34 @@
         h4[p] = send(fin.at[p], r4.at[p], yn)
         out_ref[pl.ds(pl.multiple_of(g * half_rows, half_rows), half_rows), pl.ds(p * pw, pw)] = total
 
-    for p in range(parts):
-        stage2(p)
-        if p == 1:
-            c1.wait_recv()
+    cz = []
+
+    def small(n):
+        if n == 0:
+            c0.wait_recv()
+            sb[1] = sb[0] + rb[0]
+            cz.append(send(sb.at[1], rb.at[1], xn))
+        elif n == 1:
+            cz.pop().wait_recv()
             sb[2] = sb[1] + rb[1]
-            c2 = send(sb.at[2], rb.at[2], yn)
-    for p in range(parts):
-        stage3(p)
-        if p == 1:
-            c2.wait_recv()
+            cz.append(send(sb.at[2], rb.at[2], yn))
+        elif n == 2:
+            cz.pop().wait_recv()
             sb[3] = sb[2] + rb[2]
             rz[z] = sb[3]
-            cz = []
             for k in range(1, nz):
                 to = lax.rem(z + k, nz)
                 cz.append(send(sb.at[3], rz.at[z], at(g, to, x, core)))
-    for p in range(parts):
-        stage4(p)
+
+    stages = (stage1, stage2, stage3, stage4)
+    lag = (0, 2, 3, 5)
+    for step in range(PAIRS + lag[-1]):
+        for stage, behind in zip(stages, lag):
+            q = step - behind
+            if 0 <= q < PAIRS:
+                stage(2 * q)
+                stage(2 * q + 1)
+        small(step - 1)
     for cp in cz:
         cp.wait_recv()
     total = rz[0]
@@ -431,7 +484,7 @@
     return (grad, small[0], small[1])
 
 
-SEMS = 64
+SEMS = 112
 
 
 def fits(mesh, args):

time: 136 us -> 130 us (0.956)
  the two profiles are of different devices: /device:TPU:24 before, /device:TPU:0 now
where the time goes in v2:
time: 130 us; the launch traced here: 129 us
  Pallas kernels  124 us (95%)
  local copies, waits for them, and re-layouts  3.11 us (2%)
    pallas_call x1, Pallas kernels, shards_fused(): pl.pallas_call(functools.partial(fused, fsdp_count, rp), out_shape=(jax.S...  124 us

profile of v2, /device:TPU:0, one launch (start us, length us, event | category | flops | bytes accessed | tf_op | source)
XLA Modules:
  0.0 129.2 jit_solution(3174893969620178440)
XLA Ops:
  1.3 0.6 fusion.live_ref
  1.9 124.2 %shard_map.121 = (f32[64,1024]{1,0:T(8,128)}, f32[8,1024]{1,0:T(8,128)}) custom-call(bf16[640,2048]{1,0:T(8,128)(2,1)} %t_ref.1, bf16[640,1024]{1,0:T(8,128)(2,1)} %s_ref.1, f32[5,128]{1,0:T(8,128)} %fusion.live_ref, bf16[2048,128]{1,0:T(8,128)(2,1)} %w_ref.1, f32[32,1,128]{2,1,0:T(1,128)} %bitcast.9, f32[32,1,128]{2,1,0:T(1,128)} %bitcast.10, ...), custom_call_target="tpu_custom_call" | custom-call | tf_op jit(solution)/shard_map/pallas_call | solution.py:439
  126.1 1.4 %fusion.1 = (f32[1,1024]{1,0:T(1,128)}, f32[1,1024]{1,0:T(1,128)}) fusion(f32[8,1024]{1,0:T(8,128)} %get-tuple-element.6), kind=kLoop, calls=%fused_computation.2 | loop fusion | bytes 16384 | tf_op jit(solution)/shard_map/slice | solution.py:484
  127.6 1.7 %copy.15 = f32[64,1024]{1,0:T(8,128)} copy(f32[64,1024]{1,0:T(8,128)} %get-tuple-element.12) | data formatting | bytes 524288
